TPU v7x, 256 devices: a whole 4x4x8 slice. The times are simulated.
256 devices in a mesh: blk: 64 (over x, z, core), head: 4 (over y).
Axes of the slice: x: 4, y: 4, z: 8, core: 2. Of those that a mesh axis runs over, the one named last changes fastest.
Arguments:
- ctx_q: bfloat16 [65536, 4096], P('blk', 'head'), may hold values from -120 to 120, as said below
- ctx_k: bfloat16 [65536, 1024], P('blk', 'head'), may hold values from -6 to 6
- ctx_v: bfloat16 [65536, 1024], P('blk', 'head'), may hold values from -6 to 6
- query_q: bfloat16 [64, 256, 4096], P('blk', None, 'head'), may hold values from -120 to 120, as said below
- query_k: bfloat16 [64, 256, 1024], P('blk', None, 'head'), may hold values from -6 to 6
- query_v: bfloat16 [64, 256, 1024], P('blk', None, 'head'), may hold values from -6 to 6
- out_weight: bfloat16 [4096, 4096], P('head', 'blk'), may hold values from -0.09375 to 0.09375
- anchor_index: int32 [1], replicated, may hold values from 0 to 63
- owner_index: int32 [1], replicated, may hold values from 0 to 63
- counts: int32 [64], replicated, may hold values from 256 to 1024, as said below
Outputs:
- ctx_out: bfloat16 [65536, 4096], P('blk', 'head')
- answer: bfloat16 [256, 4096], P(None, 'blk')
Inputs may be any that keep to these rules, and one draw needn't show every extreme that they name: `ctx_q`: row 5 mod 64 of a block or query slab may be a large multiple of a key row of the same head nearby. `query_q`: row 5 mod 64 of a slab may be a large multiple of a key row of the same head nearby. `counts`: some block has exactly 1024 valid tokens.
All inputs are finite; a program needn't handle non-finite values.
Results may differ from a plain program's by a relative error of at most 0.0056.
Values may be sent and summed in bfloat16 or wider, within the bound.
A program may use at most 128 MiB of HBM per device.

v0:
```python
import math

import jax
import jax.numpy as jnp
from jax import lax
from jax.sharding import Mesh
from jax.sharding import PartitionSpec as P

HEADS = 32
KV_HEADS = 8
HEAD_DIM = 128
BLK = ("blk_0", "blk_1", "blk_2")


def from_root(value, axis, source):
    kept = jnp.where(lax.axis_index(axis) == source, value, 0).astype(value.dtype)
    return lax.psum(kept, axis)


def copy_for_each(x, axis):
    length = lax.axis_size(axis)
    return lax.all_to_all(jnp.broadcast_to(x[None], (length, *x.shape)), axis, 0, 0, tiled=True)


def of_everyone(x, axis):
    return copy_for_each(x, axis).max(axis=0)


def cut_along(x, dim, length):
    before, after = (x.shape[:dim], x.shape[dim + 1 :])
    return jnp.moveaxis(x.reshape(*before, length, -1, *after), dim, 0)


def sum_at_owner(x, axis, dim):
    length = lax.axis_size(axis)
    parts = lax.all_to_all(cut_along(x, dim, length), axis, 0, 0, tiled=True)
    return jnp.sum(parts, axis=0)


def summed_rows(x, axes, dim):
    far, near = axes
    own = sum_at_owner(cut_along(x, dim, lax.axis_size(far)), near, dim + 1)
    return jnp.sum(lax.all_to_all(own, far, 0, 0, tiled=True), axis=0)


def in_one_piece(arrays, axis, dim, along):
    widths = [math.prod(a.shape[along:]) for a in arrays]
    both = jnp.concatenate(
        [a.reshape(*a.shape[:along], w) for a, w in zip(arrays, widths)], axis=along
    )
    filled = summed_rows(both, axis, dim)
    parts = jnp.split(filled, [sum(widths[:k]) for k in range(1, len(widths))], axis=along)
    return tuple(
        (b.reshape(*filled.shape[:along], *a.shape[along:]) for a, b in zip(arrays, parts))
    )


def joined_along(parts, dim):
    parts = jnp.moveaxis(parts, 0, dim)
    dims = parts.shape
    return parts.reshape(*dims[:dim], dims[dim] * dims[dim + 1], *dims[dim + 2 :])


def collect(x, axis, dim):
    return joined_along(copy_for_each(x, axis), dim)


def of_everyone_2(x, axis):
    return copy_for_each(x, axis).sum(axis=0)


def attend(queries, keys, values, mask):
    scale = HEAD_DIM ** (-0.5)
    qh = queries.transpose(1, 0, 2, 3)
    kh = keys.transpose(1, 0, 2)
    vh = values.transpose(1, 0, 2)

    def one_head(item):
        qa, ka, va = item
        scores = jnp.einsum("rgd,kd->grk", qa, ka, preferred_element_type=jnp.float32) * scale
        scores = jnp.where(mask[None], scores, -1e30)
        top = jnp.max(scores, axis=-1)
        weights = jnp.where(mask[None], jnp.exp(scores - top[..., None]), 0.0)
        total = jnp.sum(weights, axis=-1)
        summed = jnp.einsum(
            "grk,kd->grd", weights.astype(jnp.bfloat16), va, preferred_element_type=jnp.float32
        )
        return (top, total, summed)

    return lax.map(one_head, (qh, kh, vh))


def per_device(
    ctx_q, ctx_k, ctx_v, query_q, query_k, query_v, out_weight, anchor_index, owner_index, counts
):
    rows = ctx_q.shape[0]
    kv_local = ctx_k.shape[1] // HEAD_DIM
    group = HEADS // KV_HEADS
    block_id = lax.axis_index(BLK)
    anchor = anchor_index[0]
    owner = owner_index[0]
    anchor_k, anchor_v = (from_root(ctx_k, BLK, anchor), from_root(ctx_v, BLK, anchor))
    query = from_root(query_q[0], BLK, owner)
    own_count = counts[block_id]
    anchor_count = counts[anchor]
    queries = ctx_q.reshape(rows, kv_local, group, HEAD_DIM)
    keys = jnp.concatenate([anchor_k, ctx_k], axis=0).reshape(2 * rows, kv_local, HEAD_DIM)
    values = jnp.concatenate([anchor_v, ctx_v], axis=0).reshape(2 * rows, kv_local, HEAD_DIM)
    row_pos = jnp.arange(rows, dtype=jnp.int32)[:, None]
    col = jnp.arange(2 * rows, dtype=jnp.int32)[None, :]
    inner = col - rows
    mask = jnp.where(
        col < rows,
        (col < anchor_count) & (block_id != anchor),
        (inner <= row_pos) & (inner < own_count),
    )
    top, total, summed = attend(queries, keys, values, mask)
    normed = (summed / total[..., None]).transpose(2, 0, 1, 3).reshape(rows, -1)
    ctx_out = jnp.where(row_pos < own_count, normed, 0.0).astype(jnp.bfloat16)
    qrows = query.shape[0]
    query_heads = query.reshape(qrows, kv_local, group, HEAD_DIM)
    keys_two = jnp.concatenate([ctx_k, query_k[0]], axis=0).reshape(
        rows + qrows, kv_local, HEAD_DIM
    )
    values_two = jnp.concatenate([ctx_v, query_v[0]], axis=0).reshape(
        rows + qrows, kv_local, HEAD_DIM
    )
    qpos = jnp.arange(qrows, dtype=jnp.int32)[:, None]
    col_two = jnp.arange(rows + qrows, dtype=jnp.int32)[None, :]
    inner_two = col_two - rows
    mask_two = jnp.where(
        col_two < rows, col_two < own_count, (inner_two <= qpos) & (block_id == owner)
    )
    part_top, part_total, part_sum = attend(query_heads, keys_two, values_two, mask_two)
    whole_top = of_everyone(part_top, BLK)
    factor = jnp.exp(part_top - whole_top)
    flat_total = (part_total * factor).reshape(-1)
    flat_sum = (part_sum * factor[..., None]).reshape(-1, HEAD_DIM)
    share_total, share_sum = in_one_piece(
        (flat_total, flat_sum), (("blk_0", "blk_1"), "blk_2"), 0, 1
    )
    share = (share_sum / share_total[:, None]).astype(jnp.bfloat16)
    gathered = collect(share, BLK, 0)
    attn = (
        gathered.reshape(kv_local, group, qrows, HEAD_DIM).transpose(2, 0, 1, 3).reshape(qrows, -1)
    )
    partial_value = jnp.dot(attn, out_weight, preferred_element_type=jnp.float32)
    answer = of_everyone_2(partial_value, "head").astype(jnp.bfloat16)
    return (ctx_out, answer)


def solution(mesh):
    torus = Mesh(
        mesh.devices.reshape(4, 8, 2, mesh.shape["head"]), ("blk_0", "blk_1", "blk_2", "head")
    )
    placed = (
        P(BLK, "head"),
        P(BLK, "head"),
        P(BLK, "head"),
        P(BLK, None, "head"),
        P(BLK, None, "head"),
        P(BLK, None, "head"),
        P("head", BLK),
        P(),
        P(),
        P(),
    )
    return jax.shard_map(
        per_device,
        mesh=torus,
        in_specs=placed,
        out_specs=(P(BLK, "head"), P(None, BLK)),
        check_vma=False,
    )
```

profile of v0, /device:TPU:1, one launch (start us, length us, event | category | flops | bytes accessed | tf_op | source)
XLA Modules:
  0.0 394.7 jit_solution(3924606668664194695)
XLA Ops:
  8.7 1.3 copy.153
  9.9 1.2 copy.156
  11.2 1.2 copy.164
  16.8 189.2 %all-reduce.3.cloned.1.call-done = (bf16[1024,256]{0,1:T(8,128)(2,1)}, bf16[1024,256]{0,1:T(8,128)(2,1)}, bf16[2,256,4,128]{1,3,2,0:T(8,128)(2,1)}) async-done(((bf16[1024,256]{0,1:T(8,128)(2,1)}, bf16[1024,256]{0,1:T(8,128)(2,1)}, bf16[2,256,4,128]{1,3,2,0:T(8,128)(2,1)}), (bf16[1024,256]{0,1:T(8,128)(2,1)}, bf16[1024,256]{0,1:T(8,128)(2,1)}, ...) | async-done | bytes 1572880 | tf_op jit(solution)/shard_map/psum | solution.py:17
  206.0 11.3 %while.29 = (s32[]{:T(128)}, f32[2,4,256]{2,1,0:T(4,128)S(1)}, f32[2,4,256]{2,1,0:T(4,128)S(1)}, f32[2,4,256,128]{3,2,1,0:T(8,128)S(1)}, bf16[2,1280,128]{1,2,0:...) while((s32[]{:T(128)}, f32[2,4,256]{2,1,0:T(4,128)S(1)}, ...), condition=%wide.region_10.11_spmd.clone, body=%wide.region_7.10_spmd.clone.sunk | while | flops 683866112 | bytes 21145244 | solution.py:90
  207.0 2.0 fusion.108
  210.1 1.5 fusion.110
  212.7 2.0 fusion.108
  215.8 1.5 fusion.110
  217.4 26.8 %all_to_all.25 = f32[64,2,4,256]{3,2,1,0:T(4,128)S(1)} all-to-all(f32[64,2,4,256]{3,2,1,0:T(4,128)S(1)} %broadcast_in_dim.158), channel_id=1, replica_groups=mesh['blk_0'=4,'blk_1'=8,'blk_2'=2,'head'=4] {'blk_0','blk_1','blk_2'}, dimensions={0} | all-to-all | bytes 1048576 | tf_op jit(solution)/shard_map/all_to_all | solution.py:22
  246.5 5.3 %all_to_all.26 = f32[2,32,32,129]{3,2,1,0:T(8,128)S(1)} all-to-all(f32[2,32,32,129]{3,2,1,0:T(8,128)S(1)} %copy.172), channel_id=1, replica_groups=mesh['blk_0'=4,'blk_1'=8,'blk_2'=2,'head'=4] {'blk_2'}, dimensions={0} | all-to-all | bytes 2113536 | tf_op jit(solution)/shard_map/all_to_all | solution.py:36
  251.8 1.3 reduce_sum.45
  253.1 5.6 %all-to-all-start.2 = ((f32[32,32,129]{2,1,0:T(8,128)}), f32[32,32,129]{2,1,0:T(8,128)S(1)}, u32[]{:S(2)}, u32[]{:S(2)}) async-start(f32[32,32,129]{2,1,0:T(8,128)} %reduce_sum.45), calls=%async_computation.2 | async-start | bytes 2097152 | tf_op jit(solution)/shard_map/all_to_all | solution.py:43
  258.7 3.9 copy.155
  262.7 1.2 iota_compare_fusion.6
  266.2 2.1 pad_maximum_fusion.1
  268.3 15.6 %all-to-all-done.2 = f32[32,32,129]{2,1,0:T(8,128)S(1)} async-done(((f32[32,32,129]{2,1,0:T(8,128)}), f32[32,32,129]{2,1,0:T(8,128)S(1)}, u32[]{:S(2)}, u32[]{:S(2)}) %all-to-all-start.2) | async-done | bytes 528416 | tf_op jit(solution)/shard_map/all_to_all | solution.py:43
  285.1 9.8 %all-to-all-start.3 = ((bf16[64,32,128]{2,1,0:T(8,128)(2,1)}), bf16[64,32,128]{2,1,0:T(8,128)(2,1)}, u32[]{:S(2)}, u32[]{:S(2)}) async-start(bf16[64,32,128]{2,1,0:T(8,128)(2,1)} %broadcast_in_dim.159), calls=%async_computation.3 | async-start | bytes 1048576 | tf_op jit(solution)/shard_map/all_to_all | solution.py:22
  294.9 71.4 %while.28 = (s32[]{:T(128)}, f32[2,4,1024]{2,1,0:T(4,128)S(1)}, f32[2,4,1024,128]{3,2,1,0:T(8,128)}, bf16[2,2048,128]{1,2,0:T(8,128)(2,1)S(1)}, bf16[2,1024,4,12...) while((s32[]{:T(128)}, f32[2,4,1024]{2,1,0:T(4,128)S(1)}, ...), condition=%wide.region_5.6_spmd.clone, body=%wide.region_2.0_spmd.clone.sunk | while | flops 4351592448 | bytes 44105848 | solution.py:90
  295.1 2.5 fusion.103
  297.6 21.4 %fusion.104 = (f32[4,1024]{1,0:T(4,128)S(1)}, bf16[4,1024,2048]{1,2,0:T(8,128)(2,1)}) fusion(pred[1024,2048]{0,1:T(8,128)(4,1)S(1)} %fusion.103, bf16[2,1024,4,128]{1,3,2,0:T(8,128)(2,1)} %get-tuple-element.523, s32[]{:T(128)S(6)} %copy.194, bf16[2,2048,128]{1,2,0:T(8,128)(2,1)S(1)} %get-tuple-element.522), kind=kOutput, calls=%fused_computation.82.clone.1 | convolution fusion | flops 2197817344 | bytes 22561792 | tf_op jit(solution)/shard_map/while/body/eval_jaxpr/sub | solution.py:83
  319.0 11.8 %bitcast_dynamic-update-slice_fusion.8 = f32[2,4,1024,128]{3,2,1,0:T(8,128)} fusion(f32[2,4,1024,128]{3,2,1,0:T(8,128)} %get-tuple-element.510, s32[]{:T(128)S(6)} %copy.194, bf16[4,1024,2048]{1,2,0:T(8,128)(2,1)} %get-tuple-element.481, bf16[2,2048,128]{1,2,0:T(8,128)(2,1)} %get-tuple-element.524), kind=kOutput, calls=%fused_computation.15.clone.1 | convolution fusion | flops 2147483648 | bytes 19399680 | tf_op jit(solution)/shard_map/while/body/eval_jaxpr/grk,kd->grd/dot_general | solution.py:85
  330.7 2.5 fusion.103
  333.2 21.4 %fusion.104 = (f32[4,1024]{1,0:T(4,128)S(1)}, bf16[4,1024,2048]{1,2,0:T(8,128)(2,1)}) fusion(pred[1024,2048]{0,1:T(8,128)(4,1)S(1)} %fusion.103, bf16[2,1024,4,128]{1,3,2,0:T(8,128)(2,1)} %get-tuple-element.523, s32[]{:T(128)S(6)} %copy.194, bf16[2,2048,128]{1,2,0:T(8,128)(2,1)S(1)} %get-tuple-element.522), kind=kOutput, calls=%fused_computation.82.clone.1 | convolution fusion | flops 2197817344 | bytes 22561792 | tf_op jit(solution)/shard_map/while/body/eval_jaxpr/sub | solution.py:83
  354.6 11.7 %bitcast_dynamic-update-slice_fusion.8 = f32[2,4,1024,128]{3,2,1,0:T(8,128)} fusion(f32[2,4,1024,128]{3,2,1,0:T(8,128)} %get-tuple-element.510, s32[]{:T(128)S(6)} %copy.194, bf16[4,1024,2048]{1,2,0:T(8,128)(2,1)} %get-tuple-element.481, bf16[2,2048,128]{1,2,0:T(8,128)(2,1)} %get-tuple-element.524), kind=kOutput, calls=%fused_computation.15.clone.1 | convolution fusion | flops 2147483648 | bytes 19399680 | tf_op jit(solution)/shard_map/while/body/eval_jaxpr/grk,kd->grd/dot_general | solution.py:85
  366.3 2.9 divide_bitcast_fusion
  369.2 2.9 copy.161
  372.1 3.2 reshape.90
  375.4 1.2 copy.173
  377.6 4.0 %all-to-all-start.4 = ((f32[4,256,64]{1,2,0:T(8,128)}), f32[4,256,64]{1,2,0:T(8,128)S(1)}, u32[]{:S(2)}, u32[]{:S(2)}) async-start(f32[4,256,64]{1,2,0:T(8,128)} %broadcast_in_dim.160), calls=%async_computation.4 | async-start | bytes 524288 | tf_op jit(solution)/shard_map/all_to_all | solution.py:22
  381.6 1.7 select_convert_fusion
  383.3 3.9 all-to-all-done.4
  (56 shorter events, 16.1 us)
Async XLA Ops:
  7.2 369.5 %copy-start = (bf16[1024,64]{0,1:T(8,128)(2,1)S(1)}, bf16[1024,64]{0,1:T(8,128)(2,1)}, u32[]{:S(2)}) copy-start(bf16[1024,64]{0,1:T(8,128)(2,1)} %param.20) | copy-start | bytes 393220
  7.2 7.2 %copy-start.2 = (bf16[1,256,256]{2,1,0:T(8,128)(2,1)S(1)}, bf16[1,256,256]{2,1,0:T(8,128)(2,1)}, u32[]{:S(2)}) copy-start(bf16[1,256,256]{2,1,0:T(8,128)(2,1)} %param.18) | copy-start | bytes 393220
  7.2 7.3 %copy-start.3 = (bf16[1,256,256]{2,1,0:T(8,128)(2,1)S(1)}, bf16[1,256,256]{2,1,0:T(8,128)(2,1)}, u32[]{:S(2)}) copy-start(bf16[1,256,256]{2,1,0:T(8,128)(2,1)} %param.19) | copy-start | bytes 393220
  7.2 198.8 %all-reduce.3.cloned.1.call-start = ((), (), s32[]{:S(2)}) async-start(), calls=%async_computation.5 | async-start | bytes 3145728 | tf_op jit(solution)/shard_map/psum | solution.py:17
  8.6 6.0 %copy-start.4 = (s32[64]{0:T(128)S(1)}, s32[64]{0:T(128)}, u32[]{:S(2)}) copy-start(s32[64]{0:T(128)} %param.23) | copy-start | bytes 772
  209.0 1.1 copy-start.1
  214.7 1.1 copy-start.1
  253.1 30.9 %all-to-all-start.2 = ((f32[32,32,129]{2,1,0:T(8,128)}), f32[32,32,129]{2,1,0:T(8,128)S(1)}, u32[]{:S(2)}, u32[]{:S(2)}) async-start(f32[32,32,129]{2,1,0:T(8,128)} %reduce_sum.45), calls=%async_computation.2 | async-start | bytes 2097152 | tf_op jit(solution)/shard_map/all_to_all | solution.py:43
  285.1 90.3 %all-to-all-start.3 = ((bf16[64,32,128]{2,1,0:T(8,128)(2,1)}), bf16[64,32,128]{2,1,0:T(8,128)(2,1)}, u32[]{:S(2)}, u32[]{:S(2)}) async-start(bf16[64,32,128]{2,1,0:T(8,128)(2,1)} %broadcast_in_dim.159), calls=%async_computation.3 | async-start | bytes 1048576 | tf_op jit(solution)/shard_map/all_to_all | solution.py:22
  372.1 9.5 %copy-start.5 = (pred[1024]{0:T(1024)(128)(4,1)S(1)}, pred[1024]{0:T(1024)(128)(4,1)}, u32[]{:S(2)}) copy-start(pred[1024]{0:T(1024)(128)(4,1)} %iota_compare_fusion.6) | copy-start | bytes 3076
  377.6 9.7 %all-to-all-start.4 = ((f32[4,256,64]{1,2,0:T(8,128)}), f32[4,256,64]{1,2,0:T(8,128)S(1)}, u32[]{:S(2)}, u32[]{:S(2)}) async-start(f32[4,256,64]{1,2,0:T(8,128)} %broadcast_in_dim.160), calls=%async_computation.4 | async-start | bytes 524288 | tf_op jit(solution)/shard_map/all_to_all | solution.py:22
Sparse Core Ops, SparseCore 0:
  14.5 191.4 all-reduce.2
where the time goes:
time: 397 us; the launch traced here: 395 us
  waiting for transfers between devices  209 us (53%)
  matrix products  73.4 us (18%)
  blocking collectives  32.1 us (8%)
  other arithmetic  25.8 us (6%)
  starting transfers between devices  19.5 us (5%)
  local copies, waits for them, and re-layouts  19.2 us (5%)
  between operations  15.7 us (4%)
    psum x1, waiting for transfers between devices, from_root(): return lax.psum(kept, axis)  189 us
    sub x2, matrix products, one_head(): weights = jnp.where(mask[None], jnp.exp(scores - top[..., None]), 0.0)  42.7 us
    all_to_all x1, blocking collectives, copy_for_each(): lax.all_to_all(jnp.broadcast_to(x[None], (length, *x.shape)), axis, 0, 0,...  26.8 us
    dot_general x4, matrix products, one_head(): jnp.einsum('grk,kd->grd', weights.astype(jnp.bfloat16), va, preferred_ele...  26.5 us
    all_to_all x1, waiting for transfers between devices, summed_rows(): return jnp.sum(lax.all_to_all(own, far, 0, 0, tiled=True), axis=0)  15.6 us
    all_to_all x2, starting transfers between devices, copy_for_each(): lax.all_to_all(jnp.broadcast_to(x[None], (length, *x.shape)), axis, 0, 0,...  13.8 us
  transfers between devices with their start and end apart: 4, of which 3 were waited for; matrix products, arithmetic and copies ran while one was open for 24% of the time, Pallas kernels for 0%

commit v1 on v0

v1 whole, which is shorter than its diff:
```python
import functools

import jax
import jax.numpy as jnp
from jax import lax
from jax.experimental import pallas as pl
from jax.experimental.pallas import tpu as pltpu
from jax.sharding import Mesh
from jax.sharding import PartitionSpec as P

HEADS = 32
KV_HEADS = 8
HEAD_DIM = 128
BLK = ("blk_0", "blk_1", "blk_2")
NX, NZ, NY = 4, 8, 4
ROWS = 1024
QT = 256
LOCAL_KV = 2
GROUP = 4
LOCAL_HEADS = LOCAL_KV * GROUP
NEG = -1e30
SCALE2 = HEAD_DIM**-0.5 * 1.4426950408889634
F32 = jnp.float32
BF16 = jnp.bfloat16
MESH_ID = pl.DeviceIdType.MESH
RB = 256


def where_am_i():
    return tuple(lax.axis_index(a) for a in ("blk_0", "blk_1", "blk_2", "head"))


def greet(with_y):
    x, z, c, y = where_am_i()
    barrier = pltpu.get_barrier_semaphore()
    targets = [{"blk_2": 1 - c}]
    targets += [{"blk_0": lax.rem(x + d, NX)} for d in range(1, NX)]
    targets += [{"blk_1": lax.rem(z + d, NZ)} for d in range(1, NZ)]
    if with_y:
        targets += [{"head": lax.rem(y + d, NY)} for d in range(1, NY)]
    for t in targets:
        pl.semaphore_signal(barrier, inc=1, device_id=t, device_id_type=MESH_ID)
    pl.semaphore_wait(barrier, len(targets))


class Sems:
    def __init__(self, send, recv):
        self.send, self.recv, self.used = send, recv, 0

    def copy(self, src, dst, target):
        i = self.used
        self.used += 1
        return pltpu.make_async_remote_copy(
            src_ref=src,
            dst_ref=dst,
            send_sem=self.send.at[i],
            recv_sem=self.recv.at[i],
            device_id=target,
            device_id_type=MESH_ID,
        )


def start(copies):
    for c in copies:
        c.start()
    return copies


def arrived(copies):
    for c in copies:
        c.wait_recv()


def zslice(z, wide):
    if wide:
        return (
            pl.ds(pl.multiple_of(16 * (z // 4), 16), 16),
            pl.ds(pl.multiple_of(256 * lax.rem(z, 4), 256), 256),
        )
    return pl.ds(pl.multiple_of(16 * z, 16), 16), pl.ds(0, 256)


class Spread:
    def __init__(self, sems, src, out, s0, c1, sx, c2, sz, source, wide):
        self.sems, self.src, self.out = sems, src, out
        self.s0, self.c1, self.sx, self.c2, self.sz = s0, c1, sx, c2, sz
        self.fx, self.fz, self.fc = source
        self.wide = wide
        self.half = s0.shape[1]
        self.part = sx.shape[1]
        self.x, self.z, self.c, _ = where_am_i()
        self.copies = []

    def rows_half(self, c):
        return pl.ds(pl.multiple_of(self.half * c, self.half), self.half)

    def rows_x(self, c, x):
        return pl.ds(pl.multiple_of(self.half * c + self.part * x, self.part), self.part)

    def go(self, copies):
        self.copies += copies
        self.now = start(copies)

    def step0(self):
        other = 1 - self.c
        self.go([self.sems.copy(self.src.at[self.rows_half(other)], self.s0.at[self.c], {"blk_2": other})])
        self.s0[self.c] = self.src[self.rows_half(self.c), :]

    def step1(self):
        arrived(self.now)
        self.c1[...] = self.s0[self.fc]
        out = []
        for d in range(1, NX):
            t = lax.rem(self.x + d, NX)
            out.append(self.sems.copy(self.c1.at[self.rows_x(0, t)], self.sx.at[self.x], {"blk_0": t}))
        self.go(out)
        self.sx[self.x] = self.c1[self.rows_x(0, self.x), :]

    def step2(self):
        arrived(self.now)
        self.c2[...] = self.sx[self.fx]
        out = []
        for d in range(1, NZ):
            t = lax.rem(self.z + d, NZ)
            out.append(self.sems.copy(self.c2.at[zslice(t, self.wide)], self.sz.at[self.z], {"blk_1": t}))
        self.go(out)
        self.sz[self.z] = self.c2[zslice(self.z, self.wide)]

    def own(self):
        rows, cols = zslice(self.z, self.wide)
        start_row = self.half * self.c + self.part * self.x + (16 * (self.z // 4) if self.wide else 16 * self.z)
        return pl.ds(pl.multiple_of(start_row, 16), 16), cols

    def step3(self):
        arrived(self.now)
        self.out[self.own()] = self.sz[self.fz]
        self.share_z()

    def share_z(self):
        self.go(
            [
                self.sems.copy(self.out.at[self.own()], self.out.at[self.own()], {"blk_1": lax.rem(self.z + d, NZ)})
                for d in range(1, NZ)
            ]
        )

    def step4(self):
        arrived(self.now)
        piece = self.out.at[self.rows_x(self.c, self.x)]
        self.go([self.sems.copy(piece, piece, {"blk_0": lax.rem(self.x + d, NX)}) for d in range(1, NX)])

    def step5(self):
        arrived(self.now)
        piece = self.out.at[self.rows_half(self.c)]
        self.go([self.sems.copy(piece, piece, {"blk_2": 1 - self.c})])

    def step6(self):
        arrived(self.now)

    def finish(self):
        for c in self.copies:
            c.wait_send()


def coords(i):
    return i // (2 * NZ), lax.rem(i // 2, NZ), lax.rem(i, 2)


def spread_kernel(anchor_ref, owner_ref, q_ref, k_ref, v_ref, qo_ref, ko_ref, vo_ref, *rest):
    bufs, (send, recv) = rest[:15], rest[15:]
    sems = Sems(send, recv)
    greet(False)
    owner, anchor = coords(owner_ref[0]), coords(anchor_ref[0])
    q = Spread(sems, q_ref, qo_ref, *bufs[0:5], owner, True)
    k = Spread(sems, k_ref, ko_ref, *bufs[5:10], anchor, False)
    v = Spread(sems, v_ref, vo_ref, *bufs[10:15], anchor, False)
    for step in range(7):
        for a in (q, k, v):
            getattr(a, f"step{step}")()
    for a in (q, k, v):
        a.finish()


def spread_scratch():
    q = [
        pltpu.VMEM((2, 128, 1024), BF16),
        pltpu.VMEM((128, 1024), BF16),
        pltpu.VMEM((NX, 32, 1024), BF16),
        pltpu.VMEM((32, 1024), BF16),
        pltpu.VMEM((NZ, 16, 256), BF16),
    ]
    kv = [
        pltpu.VMEM((2, 512, 256), BF16),
        pltpu.VMEM((512, 256), BF16),
        pltpu.VMEM((NX, 128, 256), BF16),
        pltpu.VMEM((128, 256), BF16),
        pltpu.VMEM((NZ, 16, 256), BF16),
    ]
    return q + kv + kv


def nt(a, b):
    return lax.dot_general(a, b, (((1,), (1,)), ((), ())), preferred_element_type=F32)


def nn(a, b):
    return lax.dot_general(a, b, (((1,), (0,)), ((), ())), preferred_element_type=F32)


def iota(shape, dim):
    return lax.broadcasted_iota(jnp.int32, shape, dim)


def one_lane(rows):
    return jnp.where(iota((rows, 128), 1) == 0, 1.0, 0.0).astype(BF16)


def widen(k_ref, v_ref, ka, va, count):
    rows = k_ref.shape[0]
    hidden = (iota((rows, 128), 1) == 0) & (iota((rows, 128), 0) >= count)
    mask = jnp.where(hidden, NEG, 0.0).astype(BF16)
    ones = jnp.ones((rows, 128), BF16)
    for h in range(LOCAL_KV):
        cols = slice(h * 128, h * 128 + 128)
        ka[h, :, 0:128] = k_ref[:, cols]
        ka[h, :, 128:256] = mask
        va[h, :, 0:128] = v_ref[:, cols]
        va[h, :, 128:256] = ones


def head_cols(kv, g):
    return pl.ds(pl.multiple_of((kv * GROUP + g) * 128, 128), 128)


def own_part(kv, rb, q_ref, ka, va, o_own, m_own):
    rows = pl.ds(rb * RB, RB)
    lo = rb * RB
    e = one_lane(RB)
    tri = iota((RB, RB), 0) >= iota((RB, RB), 1)
    for g in range(GROUP):
        hh = kv * GROUP + g
        qa = jnp.concatenate([q_ref[rows, head_cols(kv, g)], e], axis=1)
        s2 = jnp.where(tri, nt(qa, ka[kv, lo : lo + RB, :]), NEG)
        m = jnp.max(s2, axis=1, keepdims=True)
        if rb:
            s1 = nt(qa, ka[kv, 0:lo, :])
            m = jnp.maximum(m, jnp.max(s1, axis=1, keepdims=True))
        p2 = jnp.exp2((s2 - m) * SCALE2).astype(BF16)
        acc = nn(p2, va[kv, lo : lo + RB, :])
        if rb:
            p1 = jnp.exp2((s1 - m) * SCALE2).astype(BF16)
            acc += nn(p1, va[kv, 0:lo, :])
        o_own[hh, rows, :] = acc
        m_own[hh, rows, :] = jnp.broadcast_to(m, (RB, 128))


def anchor_part(kv, rb, q_ref, ka, va, o_own, m_own, out_ref, own_count):
    row0 = pl.multiple_of(rb * RB, RB)
    rows = pl.ds(row0, RB)
    e = one_lane(RB)
    seen = iota((RB, 128), 0) + row0 < own_count
    for g in range(GROUP):
        hh = kv * GROUP + g
        cols = head_cols(kv, g)
        qa = jnp.concatenate([q_ref[rows, cols], e], axis=1)
        s = nt(qa, ka[kv])
        mo = m_own[hh, rows, :]
        m = jnp.maximum(mo, jnp.max(s, axis=1, keepdims=True))
        p = jnp.exp2((s - m[:, 0:1]) * SCALE2).astype(BF16)
        acc = nn(p, va[kv])
        a = jnp.exp2((mo - m) * SCALE2)
        o = acc[:, 0:128] + a * o_own[hh, rows, 0:128]
        total = acc[:, 128:256] + a * o_own[hh, rows, 128:256]
        out_ref[rows, cols] = jnp.where(seen, o / total, 0.0).astype(BF16)


def query_part(kv, q_ref, ka, va, kqa, vqa, part, stat):
    e = one_lane(QT)
    tri = iota((QT, QT), 0) >= iota((QT, QT), 1)
    lane = iota((QT, 128), 1)
    for g in range(GROUP):
        hh = kv * GROUP + g
        cols = head_cols(kv, g)
        qa = jnp.concatenate([q_ref[:, cols], e], axis=1)
        s1 = nt(qa, ka[kv])
        s2 = jnp.where(tri, nt(qa, kqa[kv]), NEG)
        m = jnp.maximum(jnp.max(s1, axis=1, keepdims=True), jnp.max(s2, axis=1, keepdims=True))
        p1 = jnp.exp2((s1 - m) * SCALE2).astype(BF16)
        p2 = jnp.exp2((s2 - m) * SCALE2).astype(BF16)
        acc = nn(p1, va[kv]) + nn(p2, vqa[kv])
        total = acc[:, 128:256]
        part[:, cols] = (acc[:, 0:128] / total).astype(BF16)
        stat[...] = jnp.where(lane == hh, m * SCALE2 + jnp.log2(total), stat[...])


def attend_kernel(
    anchor_ref, owner_ref, counts_ref, cq, ck, cv, ak, av, q, qk, qv, out, part,
    ka, va, kaa, vaa, kqa, vqa, o_own, m_own, stat,
):
    x, z, c, y = where_am_i()
    me = (x * NZ + z) * 2 + c
    anchor, owner = anchor_ref[0], owner_ref[0]
    own_count = counts_ref[me]
    anchor_count = jnp.where(me == anchor, 0, counts_ref[anchor])
    widen(ck, cv, ka, va, own_count)
    widen(ak, av, kaa, vaa, anchor_count)
    widen(qk, qv, kqa, vqa, jnp.where(me == owner, QT, 0))
    stat[...] = jnp.zeros_like(stat)

    @pl.loop(0, LOCAL_KV)
    def _(kv):
        query_part(kv, q, ka, va, kqa, vqa, part, stat)

    part[:, 1024:1152] = pack_stat(stat[...])
    for rb in range(ROWS // RB):

        @pl.loop(0, LOCAL_KV)
        def _(kv):
            own_part(kv, rb, cq, ka, va, o_own, m_own)

    @pl.loop(0, LOCAL_KV * (ROWS // RB))
    def _(i):
        anchor_part(i // 4, lax.rem(i, 4), cq, kaa, vaa, o_own, m_own, out, own_count)


def pack_stat(lse):
    lse = jnp.where(iota(lse.shape, 1) < 8, lse, 0.0)
    hi = lse.astype(BF16).astype(F32)
    mid = (lse - hi).astype(BF16).astype(F32)
    low = (lse - hi - mid).astype(BF16).astype(F32)
    return (hi + pltpu.roll(mid, 8, 1) + pltpu.roll(low, 16, 1)).astype(BF16)


def unpack_stat(stat):
    s = stat.astype(F32)
    return s + pltpu.roll(s, 120, 1) + pltpu.roll(s, 112, 1)


def merge(parts, stats, heads):
    lses = [unpack_stat(s) for s in stats]
    top = functools.reduce(jnp.maximum, lses)
    ws = [jnp.exp2(v - top) for v in lses]
    total = functools.reduce(jnp.add, ws)
    ws = [w / total for w in ws]
    outs = []
    for h in range(heads):
        acc = 0.0
        for w, o in zip(ws, parts):
            acc += w[:, h : h + 1] * o(h).astype(F32)
        outs.append(acc)
    return outs, top + jnp.log2(total)


def heads_of(ref, rows):
    return lambda h: ref[rows, h * 128 : h * 128 + 128]


class Combine:
    def __init__(self, sems, part, r0, p1, r1, p2, s2, r2o, r2s, attn):
        self.sems, self.part = sems, part
        self.r0, self.p1, self.r1, self.p2, self.s2, self.r2o, self.r2s = r0, p1, r1, p2, s2, r2o, r2s
        self.attn = attn
        self.x, self.z, self.c, self.y = where_am_i()
        self.copies = []

    def go(self, copies):
        self.copies += copies
        self.now = start(copies)

    def step0(self):
        other = 1 - self.c
        rows = pl.ds(pl.multiple_of(128 * other, 128), 128)
        self.go([self.sems.copy(self.part.at[rows], self.r0, {"blk_2": other})])

    def step1(self):
        arrived(self.now)
        lo = pl.multiple_of(128 * self.c, 128)

        @pl.loop(0, 4)
        def _(i):
            mine = pl.ds(pl.multiple_of(lo + 32 * i, 32), 32)
            theirs = pl.ds(pl.multiple_of(32 * i, 32), 32)
            outs, lse = merge(
                [heads_of(self.part, mine), heads_of(self.r0, theirs)],
                [self.part[mine, 1024:1152], self.r0[theirs, 1024:1152]],
                LOCAL_HEADS,
            )
            for h, o in enumerate(outs):
                self.p1[theirs, h * 128 : h * 128 + 128] = o.astype(BF16)
            self.p1[theirs, 1024:1152] = pack_stat(lse)

        def rows(x):
            return pl.ds(pl.multiple_of(32 * x, 32), 32)

        out = []
        for d in range(1, NX):
            t = lax.rem(self.x + d, NX)
            out.append(self.sems.copy(self.p1.at[rows(t)], self.r1.at[self.x], {"blk_0": t}))
        self.go(out)
        self.r1[self.x] = self.p1[rows(self.x), :]

    def step2(self):
        arrived(self.now)
        outs, lse = merge(
            [heads_of(self.r1.at[i], slice(0, 32)) for i in range(NX)],
            [self.r1[i, :, 1024:1152] for i in range(NX)],
            LOCAL_HEADS,
        )
        for h, o in enumerate(outs):
            self.p2[:, h * 128 : h * 128 + 128] = o.astype(BF16)
        for g in range(4):
            self.s2[g] = pack_stat(pltpu.roll(lse, 128 - 2 * g, 1) if g else lse)
        out = []
        for d in range(1, NZ):
            t = lax.rem(self.z + d, NZ)
            rows, cols = zslice(t, True)
            out.append(self.sems.copy(self.p2.at[rows, cols], self.r2o.at[self.z], {"blk_1": t}))
            out.append(self.sems.copy(self.s2.at[lax.rem(t, 4), rows], self.r2s.at[self.z], {"blk_1": t}))
        self.go(out)
        rows, cols = zslice(self.z, True)
        self.r2o[self.z] = self.p2[rows, cols]
        self.r2s[self.z] = self.s2[lax.rem(self.z, 4), rows, :]


def combine_kernel(part, w, ans, r0, p1, r1, p2, s2, r2o, r2s, attn, ry, send, recv):
    sems = Sems(send, recv)
    greet(True)
    x, z, c, y = where_am_i()
    comb = Combine(sems, part, r0, p1, r1, p2, s2, r2o, r2s, attn)
    comb.step0()
    comb.step1()
    comb.step2()
    arrived(comb.now)
    outs, _ = merge(
        [heads_of(r2o.at[i], slice(0, 16)) for i in range(NZ)], [r2s[i] for i in range(NZ)], 2
    )
    share = Share(sems, attn)
    share.put(jnp.concatenate(outs, axis=1).astype(BF16))
    share.share_z()
    share.step4()
    share.step5()
    share.step6()
    project(attn, w, ry, y)
    last = [
        sems.copy(ry.at[y], ry.at[y], {"head": lax.rem(y + d, NY)}) for d in range(1, NY)
    ]
    start(last)
    arrived(last)
    answer(ry, ans)
    for cp in comb.copies + share.copies + last:
        cp.wait_send()


class Share(Spread):
    def __init__(self, sems, out):
        self.sems, self.out, self.wide = sems, out, True
        self.half, self.part = 128, 32
        self.x, self.z, self.c, _ = where_am_i()
        self.copies = []

    def put(self, value):
        self.out[self.own()] = value


def project(attn, w, ry, y):
    ry[y] = jnp.concatenate([nn(attn[0:128, :], w[...]), nn(attn[128:256, :], w[...])], axis=1)


def answer(ry, ans):
    total = ((ry[0] + ry[1]) + ry[2]) + ry[3]
    ans[0:128, :] = total[:, 0:64].astype(BF16)
    ans[128:256, :] = total[:, 64:128].astype(BF16)


VM = pl.BlockSpec(memory_space=pltpu.VMEM)
SM = pl.BlockSpec(memory_space=pltpu.SMEM)


def shape(*dims, dtype=BF16):
    return jax.ShapeDtypeStruct(dims, dtype)


def per_device(ctx_q, ctx_k, ctx_v, query_q, query_k, query_v, out_weight, anchor_index, owner_index, counts):
    q, ak, av = pl.pallas_call(
        spread_kernel,
        out_shape=(shape(QT, 1024), shape(ROWS, 256), shape(ROWS, 256)),
        in_specs=[SM, SM, VM, VM, VM],
        out_specs=(VM, VM, VM),
        scratch_shapes=spread_scratch() + [pltpu.SemaphoreType.DMA((66,)), pltpu.SemaphoreType.DMA((66,))],
        compiler_params=pltpu.CompilerParams(collective_id=0, has_side_effects=True),
        name="spread",
    )(anchor_index, owner_index, query_q[0], ctx_k, ctx_v)
    ctx_out, part = pl.pallas_call(
        attend_kernel,
        out_shape=(shape(ROWS, 1024), shape(QT, 1152)),
        in_specs=[SM, SM, SM] + [VM] * 8,
        out_specs=(VM, VM),
        scratch_shapes=[
            pltpu.VMEM((LOCAL_KV, ROWS, 256), BF16),
            pltpu.VMEM((LOCAL_KV, ROWS, 256), BF16),
            pltpu.VMEM((LOCAL_KV, ROWS, 256), BF16),
            pltpu.VMEM((LOCAL_KV, ROWS, 256), BF16),
            pltpu.VMEM((LOCAL_KV, QT, 256), BF16),
            pltpu.VMEM((LOCAL_KV, QT, 256), BF16),
            pltpu.VMEM((LOCAL_HEADS, ROWS, 256), F32),
            pltpu.VMEM((LOCAL_HEADS, ROWS, 128), F32),
            pltpu.VMEM((QT, 128), F32),
        ],
        compiler_params=pltpu.CompilerParams(),
        name="attend",
    )(anchor_index, owner_index, counts, ctx_q, ctx_k, ctx_v, ak, av, q, query_k[0], query_v[0])
    ans = pl.pallas_call(
        combine_kernel,
        out_shape=shape(QT, 64),
        in_specs=[VM, VM],
        out_specs=VM,
        scratch_shapes=[
            pltpu.VMEM((128, 1152), BF16),
            pltpu.VMEM((128, 1152), BF16),
            pltpu.VMEM((NX, 32, 1152), BF16),
            pltpu.VMEM((32, 1024), BF16),
            pltpu.VMEM((4, 32, 128), BF16),
            pltpu.VMEM((NZ, 16, 256), BF16),
            pltpu.VMEM((NZ, 16, 128), BF16),
            pltpu.VMEM((QT, 1024), BF16),
            pltpu.VMEM((NY, 128, 128), F32),
            pltpu.SemaphoreType.DMA((32,)),
            pltpu.SemaphoreType.DMA((32,)),
        ],
        compiler_params=pltpu.CompilerParams(collective_id=1, has_side_effects=True),
        name="combine",
    )(part, out_weight)
    return ctx_out, ans


def solution(mesh):
    torus = Mesh(
        mesh.devices.reshape(NX, NZ, 2, mesh.shape["head"]), ("blk_0", "blk_1", "blk_2", "head")
    )
    placed = (
        P(BLK, "head"),
        P(BLK, "head"),
        P(BLK, "head"),
        P(BLK, None, "head"),
        P(BLK, None, "head"),
        P(BLK, None, "head"),
        P("head", BLK),
        P(),
        P(),
        P(),
    )
    return jax.shard_map(
        per_device,
        mesh=torus,
        in_specs=placed,
        out_specs=(P(BLK, "head"), P(None, BLK)),
        check_vma=False,
    )
```

time: 397 us -> 120 us (0.30)
  waiting for transfers between devices: 209 us -> 0 us
  Pallas kernels: 0 us -> 115 us
  matrix products: 73.4 us -> 0 us
  blocking collectives: 32.1 us -> 0 us
  other arithmetic: 25.8 us -> 0 us
  starting transfers between devices: 19.5 us -> 0 us
  local copies, waits for them, and re-layouts: 19.2 us -> 2.39 us
  between operations: 15.7 us -> 1.95 us
    psum x1 -> x0, waiting for transfers between devices: 189 us -> none  [from_root(): return lax.psum(kept, axis)]
    pallas_call x0 -> x3, Pallas kernels: none -> 115 us  [the longest x1 42.6 us: per_device(): pl.pallas_call(spread_kernel, out_shape=(shape(QT, 1024), shape(ROWS, 256...]
    sub x2 -> x0, matrix products: 42.7 us -> none  [one_head(): weights = jnp.where(mask[None], jnp.exp(scores - top[..., None]), 0.0)]
    all_to_all x2 -> x0, blocking collectives: 32.1 us -> none  [the longest x1 26.8 us: copy_for_each(): lax.all_to_all(jnp.broadcast_to(x[None], (length, *x.shape)), axis, 0, 0,...]
    dot_general x7 -> x0, matrix products: 30.7 us -> none  [the longest x4 26.5 us: one_head(): jnp.einsum('grk,kd->grd', weights.astype(jnp.bfloat16), va, preferred_ele...]
    all_to_all x3 -> x0, waiting for transfers between devices: 19.5 us -> none  [the longest x1 15.6 us: summed_rows(): return jnp.sum(lax.all_to_all(own, far, 0, 0, tiled=True), axis=0)]
    all_to_all x3 -> x0, starting transfers between devices: 19.4 us -> none  [the longest x2 13.8 us: copy_for_each(): lax.all_to_all(jnp.broadcast_to(x[None], (length, *x.shape)), axis, 0, 0,...]
    select_n x6 -> x0, other arithmetic: 8.9 us -> none  [the longest x2 4.94 us: per_device(): jnp.where(col < rows, (col < anchor_count) & (block_id != anchor), (inner...]
  transfers between devices with their start and end apart: 4 -> 0, of which waited for: 3 -> 0; matrix products, arithmetic and copies ran while one was open for 24% -> 0% of each run, Pallas kernels for 0% -> 0%
where the time goes in v1:
time: 120 us
  Pallas kernels  115 us (96%)
  local copies, waits for them, and re-layouts  2.39 us (2%)
  between operations  1.95 us (2%)
    pallas_call x1, Pallas kernels, per_device(): pl.pallas_call(spread_kernel, out_shape=(shape(QT, 1024), shape(ROWS, 256...  42.6 us
    pallas_call x1, Pallas kernels, per_device(): pl.pallas_call(combine_kernel, out_shape=shape(QT, 64), in_specs=[VM, VM]...  38 us
    pallas_call x1, Pallas kernels, per_device(): pl.pallas_call(attend_kernel, out_shape=(shape(ROWS, 1024), shape(QT, 115...  34.8 us

profile of v1, /device:TPU:1, one launch (start us, length us, event | category | flops | bytes accessed | tf_op | source)
XLA Modules:
  0.0 119.7 jit_solution(7388432708199678315)
XLA Ops:
  1.9 42.6 %spread.1 = (bf16[256,1024]{1,0:T(8,128)(2,1)}, bf16[1024,256]{1,0:T(8,128)(2,1)}, bf16[1024,256]{1,0:T(8,128)(2,1)}) custom-call(s32[1]{0:T(128)S(6)} %copy.14.anchor_ref, s32[1]{0:T(128)S(6)} %copy.15.owner_ref, bf16[256,1024]{1,0:T(8,128)(2,1)} %bitcast.3, bf16[1024,256]{1,0:T(8,128)(2,1)} %ck.1, bf16[1024,256]{1,0:T(8,128)(2,1)} %cv.1), custom_call_target="tpu_custom_call" | custom-call | tf_op jit(solution)/shard_map/spread/pallas_call | solution.py:484
  44.5 0.0 copy-start
  44.5 34.8 %attend.1 = (bf16[1024,1024]{1,0:T(8,128)(2,1)}, bf16[256,1152]{1,0:T(8,128)(2,1)}) custom-call(s32[1]{0:T(128)S(6)} %copy.14.anchor_ref, s32[1]{0:T(128)S(6)} %copy.15.owner_ref, s32[64]{0:T(128)} %counts_ref.1, bf16[1024,1024]{1,0:T(8,128)(2,1)} %cq.1, bf16[1024,256]{1,0:T(8,128)(2,1)} %ck.1, bf16[1024,256]{1,0:T(8,128)(2,1)} %cv.1, ...), custom_call_target="tpu_custom_call" | custom-call | tf_op jit(solution)/shard_map/attend/pallas_call | solution.py:493
  79.3 0.0 copy-done
  79.3 0.8 copy.12.w
  80.1 38.0 %combine.1 = bf16[256,64]{1,0:T(8,128)(2,1)} custom-call(bf16[256,1152]{1,0:T(8,128)(2,1)} %get-tuple-element.11.part, bf16[1024,64]{1,0:T(8,128)(2,1)} %copy.12.w), custom_call_target="tpu_custom_call" | custom-call | tf_op jit(solution)/shard_map/combine/pallas_call | solution.py:512
  118.1 1.5 %copy.13 = bf16[256,64]{0,1:T(8,128)(2,1)} copy(bf16[256,64]{1,0:T(8,128)(2,1)} %combine.1) | data formatting | bytes 65536
Async XLA Ops:
  44.5 34.8 %copy-start = (bf16[1024,64]{0,1:T(8,128)(2,1)S(1)}, bf16[1024,64]{0,1:T(8,128)(2,1)}, u32[]{:S(2)}) copy-start(bf16[1024,64]{0,1:T(8,128)(2,1)} %param.16) | copy-start | bytes 393220

commit v2 on v1

v2 whole, which is shorter than its diff:
```python
import functools

import jax
import jax.numpy as jnp
from jax import lax
from jax.experimental import pallas as pl
from jax.experimental.pallas import tpu as pltpu
from jax.sharding import Mesh
from jax.sharding import PartitionSpec as P

HEADS = 32
KV_HEADS = 8
HEAD_DIM = 128
BLK = ("blk_0", "blk_1", "blk_2")
NX, NZ, NY = 4, 8, 4
SIZE = {"blk_0": NX, "blk_1": NZ}
ROWS = 1024
QT = 256
LOCAL_KV = 2
GROUP = 4
LOCAL_HEADS = LOCAL_KV * GROUP
NEG = -1e30
VMEM_LIMIT = 52 << 20
SCALE2 = HEAD_DIM**-0.5 * 1.4426950408889634
F32 = jnp.float32
BF16 = jnp.bfloat16
MESH_ID = pl.DeviceIdType.MESH
RB = 256


def where_am_i():
    return tuple(lax.axis_index(a) for a in ("blk_0", "blk_1", "blk_2", "head"))


def plane_peers():
    x, z, c, y = where_am_i()
    out = []
    for dc in range(2):
        for dx in range(NX):
            for dy in range(NY):
                if dc or dx or dy:
                    out.append((lax.rem(x + dx, NX), lax.rem(c + dc, 2), lax.rem(y + dy, NY)))
    return out


def greet():
    z = lax.axis_index("blk_1")
    barrier = pltpu.get_barrier_semaphore()
    targets = [{"blk_1": lax.rem(z + d, NZ)} for d in range(1, NZ)]
    targets += [{"blk_0": px, "blk_2": pc, "head": py} for px, pc, py in plane_peers()]
    for t in targets:
        pl.semaphore_signal(barrier, inc=1, device_id=t, device_id_type=MESH_ID)
    pl.semaphore_wait(barrier, len(targets))


class Sems:
    def __init__(self, send, recv):
        self.send, self.recv, self.used = send, recv, 0

    def copy(self, src, dst, target):
        i = self.used
        self.used += 1
        return pltpu.make_async_remote_copy(
            src_ref=src,
            dst_ref=dst,
            send_sem=self.send.at[i],
            recv_sem=self.recv.at[i],
            device_id=target,
            device_id_type=MESH_ID,
        )


def start(copies):
    for c in copies:
        c.start()
    return copies


def arrived(copies):
    for c in copies:
        c.wait_recv()


def zslice(z):
    return (
        pl.ds(pl.multiple_of(16 * (z // 4), 16), 16),
        pl.ds(pl.multiple_of(128 * lax.rem(z, 4), 128), 128),
    )


def rows_at(start, size):
    return pl.ds(pl.multiple_of(start, 16), size)


class Spread:
    def __init__(self, sems, src, out, s0, c1, sx, c2, sz, source, order, wide):
        self.sems, self.src, self.out = sems, src, out
        self.s0, self.c1, self.sx, self.c2, self.sz = s0, c1, sx, c2, sz
        self.source = source
        self.setup(order, wide, s0.shape[1])

    def setup(self, order, wide, half):
        self.order, self.wide, self.half = order, wide, half
        x, z, c, _ = where_am_i()
        self.c = c
        self.me = {"blk_0": x, "blk_1": z}
        self.first, self.second = order
        self.part = half // SIZE[self.first]
        self.copies = []

    def peers(self, axis):
        return [lax.rem(self.me[axis] + d, SIZE[axis]) for d in range(1, SIZE[axis])]

    def rows_half(self, c):
        return rows_at(self.half * c, self.half)

    def rows_part(self, c, i):
        return rows_at(self.half * c + self.part * i, self.part)

    def slice2(self, i):
        if self.wide:
            return zslice(i)
        return rows_at(16 * i, 16), pl.ds(0, 256)

    def go(self, copies):
        self.copies += copies
        self.now = start(copies)

    def step0(self):
        other = 1 - self.c
        self.go([self.sems.copy(self.src.at[self.rows_half(other)], self.s0.at[self.c], {"blk_2": other})])
        self.s0[self.c] = self.src[self.rows_half(self.c), :]

    def step1(self):
        arrived(self.now)
        self.c1[...] = self.s0[self.source["blk_2"]]
        i = self.me[self.first]
        self.go(
            [
                self.sems.copy(self.c1.at[self.rows_part(0, t)], self.sx.at[i], {self.first: t})
                for t in self.peers(self.first)
            ]
        )
        self.sx[i] = self.c1[self.rows_part(0, i), :]

    def step2(self):
        arrived(self.now)
        self.c2[...] = self.sx[self.source[self.first]]
        i = self.me[self.second]
        self.go(
            [
                self.sems.copy(self.c2.at[self.slice2(t)], self.sz.at[i], {self.second: t})
                for t in self.peers(self.second)
            ]
        )
        self.sz[i] = self.c2[self.slice2(i)]

    def own(self):
        i = self.me[self.second]
        base = self.half * self.c + self.part * self.me[self.first]
        if self.wide:
            return rows_at(base + 16 * (i // 4), 16), zslice(i)[1]
        return rows_at(base + 16 * i, 16), pl.ds(0, 256)

    def step3(self):
        arrived(self.now)
        self.out[self.own()] = self.sz[self.source[self.second]]
        self.share()

    def share(self):
        piece = self.out.at[self.own()]
        self.go([self.sems.copy(piece, piece, {self.second: t}) for t in self.peers(self.second)])

    def step4(self):
        arrived(self.now)
        piece = self.out.at[self.rows_part(self.c, self.me[self.first])]
        self.go([self.sems.copy(piece, piece, {self.first: t}) for t in self.peers(self.first)])

    def step5(self):
        arrived(self.now)
        piece = self.out.at[self.rows_half(self.c)]
        self.go([self.sems.copy(piece, piece, {"blk_2": 1 - self.c})])

    def step6(self):
        arrived(self.now)


def coords(i):
    return {"blk_0": i // (2 * NZ), "blk_1": lax.rem(i // 2, NZ), "blk_2": lax.rem(i, 2)}


def spread_scratch(rows, width, order, wide):
    half = rows // 2
    part = half // SIZE[order[0]]
    return [
        pltpu.VMEM((2, half, width), BF16),
        pltpu.VMEM((half, width), BF16),
        pltpu.VMEM((SIZE[order[0]], part, width), BF16),
        pltpu.VMEM((part, width), BF16),
        pltpu.VMEM((SIZE[order[1]], 16, 128 if wide else 256), BF16),
    ]


def nt(a, b):
    return lax.dot_general(a, b, (((1,), (1,)), ((), ())), preferred_element_type=F32)


def nn(a, b):
    return lax.dot_general(a, b, (((1,), (0,)), ((), ())), preferred_element_type=F32)


def iota(shape, dim):
    return lax.broadcasted_iota(jnp.int32, shape, dim)


def one_lane(rows):
    return jnp.where(iota((rows, 128), 1) == 0, 1.0, 0.0).astype(BF16)


def widen(k_ref, v_ref, ka, va, count):
    rows = k_ref.shape[0]
    hidden = (iota((rows, 128), 1) == 0) & (iota((rows, 128), 0) >= count)
    mask = jnp.where(hidden, NEG, 0.0).astype(BF16)
    ones = jnp.ones((rows, 128), BF16)
    for h in range(LOCAL_KV):
        cols = slice(h * 128, h * 128 + 128)
        ka[h, :, 0:128] = k_ref[:, cols]
        ka[h, :, 128:256] = mask
        va[h, :, 0:128] = v_ref[:, cols]
        va[h, :, 128:256] = ones


def head_cols(kv, g):
    return pl.ds(pl.multiple_of((kv * GROUP + g) * 128, 128), 128)


def own_part(kv, rb, q_ref, ka, va, o_own, m_own):
    rows = pl.ds(rb * RB, RB)
    lo = rb * RB
    e = one_lane(RB)
    tri = iota((RB, RB), 0) >= iota((RB, RB), 1)
    for g in range(GROUP):
        hh = kv * GROUP + g
        qa = jnp.concatenate([q_ref[rows, head_cols(kv, g)], e], axis=1)
        s2 = jnp.where(tri, nt(qa, ka[kv, lo : lo + RB, :]), NEG)
        m = jnp.max(s2, axis=1, keepdims=True)
        if rb:
            s1 = nt(qa, ka[kv, 0:lo, :])
            m = jnp.maximum(m, jnp.max(s1, axis=1, keepdims=True))
        p2 = jnp.exp2((s2 - m) * SCALE2).astype(BF16)
        acc = nn(p2, va[kv, lo : lo + RB, :])
        if rb:
            p1 = jnp.exp2((s1 - m) * SCALE2).astype(BF16)
            acc += nn(p1, va[kv, 0:lo, :])
        o_own[hh, rows, :] = acc
        m_own[hh, rows, :] = jnp.broadcast_to(m, (RB, 128))


def anchor_part(kv, rb, q_ref, ka, va, o_own, m_own, out_ref, own_count):
    row0 = pl.multiple_of(rb * RB, RB)
    rows = pl.ds(row0, RB)
    e = one_lane(RB)
    seen = iota((RB, 128), 0) + row0 < own_count
    for g in range(GROUP):
        hh = kv * GROUP + g
        cols = head_cols(kv, g)
        qa = jnp.concatenate([q_ref[rows, cols], e], axis=1)
        s = nt(qa, ka[kv])
        mo = m_own[hh, rows, :]
        m = jnp.maximum(mo, jnp.max(s, axis=1, keepdims=True))
        p = jnp.exp2((s - m[:, 0:1]) * SCALE2).astype(BF16)
        acc = nn(p, va[kv])
        a = jnp.exp2((mo - m) * SCALE2)
        o = acc[:, 0:128] + a * o_own[hh, rows, 0:128]
        total = acc[:, 128:256] + a * o_own[hh, rows, 128:256]
        out_ref[rows, cols] = jnp.where(seen, o / total, 0.0).astype(BF16)


def self_part(kv, q_ref, kqa, vqa, o_self, m_self):
    e = one_lane(QT)
    row = iota((QT, QT), 0)
    at = lax.rem(row // 16, 2) * 128 + (row // 32) * 16 + lax.rem(row, 16)
    tri = at >= iota((QT, QT), 1)
    for g in range(GROUP):
        hh = kv * GROUP + g
        qa = jnp.concatenate([q_ref[kv, :, g * 128 : g * 128 + 128], e], axis=1)
        s = jnp.where(tri, nt(qa, kqa[kv]), NEG)
        m = jnp.max(s, axis=1, keepdims=True)
        o_self[hh] = nn(jnp.exp2((s - m) * SCALE2).astype(BF16), vqa[kv])
        m_self[hh] = jnp.broadcast_to(m, (QT, 128))


def query_part(kv, q_ref, ka, va, o_self, m_self, is_owner, part, part32):
    e = one_lane(QT)
    lane = iota((QT, 128), 1)
    stat = jnp.zeros((QT, 128), F32)
    for g in range(GROUP):
        hh = kv * GROUP + g
        cols = slice(g * 128, g * 128 + 128)
        qa = jnp.concatenate([q_ref[kv, :, cols], e], axis=1)
        s = nt(qa, ka[kv])
        ms = jnp.where(is_owner, m_self[hh], NEG)
        m = jnp.maximum(ms, jnp.max(s, axis=1, keepdims=True))
        p = jnp.exp2((s - m[:, 0:1]) * SCALE2).astype(BF16)
        acc = nn(p, va[kv])
        a = jnp.exp2((ms - m) * SCALE2)
        total = acc[:, 128:256] + a * o_self[hh, :, 128:256]
        o = (acc[:, 0:128] + a * o_self[hh, :, 0:128]) / total
        part32[kv, :, cols] = o
        part[kv, :, cols] = o.astype(BF16)
        stat = jnp.where(lane == g, m * SCALE2 + jnp.log2(total), stat)
    part[kv, :, 512:640] = pack_stat(stat)


def pack_stat(lse):
    lse = jnp.where(iota(lse.shape, 1) < 8, lse, 0.0)
    hi = lse.astype(BF16).astype(F32)
    mid = (lse - hi).astype(BF16).astype(F32)
    low = (lse - hi - mid).astype(BF16).astype(F32)
    return (hi + pltpu.roll(mid, 8, 1) + pltpu.roll(low, 16, 1)).astype(BF16)


def unpack_stat(stat):
    s = stat.astype(F32)
    return s + pltpu.roll(s, 120, 1) + pltpu.roll(s, 112, 1)


def merge(parts, stats, heads):
    lses = [unpack_stat(s) for s in stats]
    top = functools.reduce(jnp.maximum, lses)
    ws = [jnp.exp2(v - top) for v in lses]
    total = functools.reduce(jnp.add, ws)
    ws = [w / total for w in ws]
    outs = []
    for h in range(heads):
        acc = 0.0
        for w, o in zip(ws, parts):
            acc += w[:, h : h + 1] * o(h).astype(F32)
        outs.append(acc)
    return outs, top + jnp.log2(total)


def heads_of(ref, rows):
    return lambda h: ref[rows, h * 128 : h * 128 + 128]


class Combine:
    def __init__(self, sems, part, part32, r0, p1, p1f, r1, p2, p2f, s2, r2o, r2s):
        self.sems, self.part, self.part32 = sems, part, part32
        self.r0, self.p1, self.p1f, self.r1 = r0, p1, p1f, r1
        self.p2, self.p2f, self.s2, self.r2o, self.r2s = p2, p2f, s2, r2o, r2s
        self.x, self.z, self.c, self.y = where_am_i()
        self.copies = []

    def go(self, copies):
        self.copies += copies
        self.now = start(copies)

    def step0(self):
        other = 1 - self.c
        self.go([self.sems.copy(self.part.at[rows_at(128 * other, 128)], self.r0, {"blk_2": other})])

    def step1(self):
        arrived(self.now)

        @pl.loop(0, 4)
        def _(i):
            mine = rows_at(128 * self.c + 32 * i, 32)
            theirs = rows_at(32 * i, 32)
            outs, lse = merge(
                [heads_of(self.part32, mine), heads_of(self.r0, theirs)],
                [self.part[mine, 512:640], self.r0[theirs, 512:640]],
                GROUP,
            )
            for h, o in enumerate(outs):
                self.p1[theirs, h * 128 : h * 128 + 128] = o.astype(BF16)
                self.p1f[theirs, h * 128 : h * 128 + 128] = o
            self.p1[theirs, 512:640] = pack_stat(lse)

        out = []
        for d in range(1, NX):
            t = lax.rem(self.x + d, NX)
            out.append(self.sems.copy(self.p1.at[rows_at(32 * t, 32)], self.r1.at[d - 1], {"blk_0": t}))
        self.go(out)

    def step2(self):
        arrived(self.now)
        mine = rows_at(32 * self.x, 32)
        outs, lse = merge(
            [heads_of(self.p1f, mine)] + [heads_of(self.r1.at[i], slice(0, 32)) for i in range(NX - 1)],
            [self.p1[mine, 512:640]] + [self.r1[i, :, 512:640] for i in range(NX - 1)],
            GROUP,
        )
        for h, o in enumerate(outs):
            self.p2[:, h * 128 : h * 128 + 128] = o.astype(BF16)
            self.p2f[:, h * 128 : h * 128 + 128] = o
        for g in range(4):
            self.s2[g] = pack_stat(pltpu.roll(lse, 128 - g, 1) if g else lse)
        out = []
        for d in range(1, NZ):
            t = lax.rem(self.z + d, NZ)
            rows, cols = zslice(t)
            out.append(self.sems.copy(self.p2.at[rows, cols], self.r2o.at[d - 1], {"blk_1": t}))
            out.append(self.sems.copy(self.s2.at[lax.rem(t, 4), rows], self.r2s.at[d - 1], {"blk_1": t}))
        self.go(out)

    def step3(self):
        arrived(self.now)
        rows, cols = zslice(self.z)
        own = self.p2f[rows, cols]
        outs, _ = merge(
            [lambda h: own[:, h * 128 : h * 128 + 128]]
            + [heads_of(self.r2o.at[i], slice(0, 16)) for i in range(NZ - 1)],
            [self.s2[lax.rem(self.z, 4), rows, :]] + [self.r2s[i] for i in range(NZ - 1)],
            1,
        )
        return outs[0].astype(BF16)


class Share(Spread):
    def __init__(self, sems, out):
        self.sems, self.out = sems, out
        self.setup(("blk_0", "blk_1"), True, 128)

    def own(self):
        return zslice(self.me["blk_1"])


def project(attn, wall, sb):
    rows = jnp.concatenate([attn[0], attn[1]], axis=1)
    p = nt(rows, wall[...].reshape(512, 1024))
    for i in range(8):
        cols = slice(i * 64, i * 64 + 64)
        sb[i] = jnp.concatenate([p[0:16, cols], p[16:32, cols]], axis=1)


def answer(rf, ans):
    total = (((rf[0] + rf[1]) + rf[2]) + rf[3]).reshape(128, 128).T
    ans[:, 0:128] = total[0:64].astype(BF16)
    ans[:, 128:256] = total[64:128].astype(BF16)


XZ = ("blk_0", "blk_1")
ZX = ("blk_1", "blk_0")
N_LOCAL = 11
SCALARS = ("anchor", "owner", "counts")
N_REMOTE = 4 * 22 + 2 * (1 + 3 + 14 + 7) + 4 + 31


def scratch_list():
    kva = pltpu.VMEM((LOCAL_KV, ROWS, 256), BF16)
    kvq = pltpu.VMEM((LOCAL_KV, QT, 256), BF16)
    named = dict(
        cq=pltpu.VMEM((ROWS, 1024), BF16),
        ck=pltpu.VMEM((ROWS, 256), BF16),
        cv=pltpu.VMEM((ROWS, 256), BF16),
        q=pltpu.VMEM((2, QT, 512), BF16),
        qk=pltpu.VMEM((QT, 256), BF16),
        qv=pltpu.VMEM((QT, 256), BF16),
        wall=pltpu.VMEM((2, NX, 64, 1024), BF16),
        qo=pltpu.VMEM((2, QT, 512), BF16),
        ko=pltpu.VMEM((ROWS, 256), BF16),
        vo=pltpu.VMEM((ROWS, 256), BF16),
        ka=kva, va=kva, kaa=kva, vaa=kva, kqa=kvq, vqa=kvq,
        o_own=pltpu.VMEM((LOCAL_HEADS, ROWS, 256), F32),
        m_own=pltpu.VMEM((LOCAL_HEADS, ROWS, 128), F32),
        o_self=pltpu.VMEM((LOCAL_HEADS, QT, 256), F32),
        m_self=pltpu.VMEM((LOCAL_HEADS, QT, 128), F32),
        part=pltpu.VMEM((2, QT, 640), BF16),
        part32=pltpu.VMEM((2, QT, 512), F32),
        r0=pltpu.VMEM((2, 128, 640), BF16),
        p1=pltpu.VMEM((2, 128, 640), BF16),
        p1f=pltpu.VMEM((2, 128, 512), F32),
        r1=pltpu.VMEM((2, NX - 1, 32, 640), BF16),
        p2=pltpu.VMEM((2, 32, 512), BF16),
        p2f=pltpu.VMEM((2, 32, 512), F32),
        s2=pltpu.VMEM((2, 4, 32, 128), BF16),
        r2o=pltpu.VMEM((2, NZ - 1, 16, 128), BF16),
        r2s=pltpu.VMEM((2, NZ - 1, 16, 128), BF16),
        attn=pltpu.VMEM((2, 32, 512), BF16),
        sb=pltpu.VMEM((8, 16, 128), F32),
        rf=pltpu.VMEM((NY, 8, 16, 128), F32),
        anchor=pltpu.SMEM((1,), jnp.int32),
        owner=pltpu.SMEM((1,), jnp.int32),
        counts=pltpu.SMEM((64,), jnp.int32),
        local=pltpu.SemaphoreType.DMA((N_LOCAL,)),
        send=pltpu.SemaphoreType.DMA((N_REMOTE,)),
        recv=pltpu.SemaphoreType.DMA((N_REMOTE,)),
    )
    return named


def layer_kernel(*refs):
    scalars, inputs, (out_vmem, ans), rest = refs[:3], refs[3:10], refs[10:12], refs[12:]
    names = scratch_list()
    b = dict(zip(names, rest))
    bufs = rest[len(names) :]
    x, z, c, y = where_am_i()
    slot = c * NX + x
    local = b["local"]
    q_hbm = inputs[0]
    q_whole = []
    for kv in range(2):
        cols = pl.ds(512 * kv, 512)
        for i in range(8):
            for hi in range(2):
                pltpu.make_async_copy(
                    q_hbm.at[pl.ds(128 * hi + 16 * i, 16), cols],
                    b["q"].at[kv, pl.ds(32 * i + 16 * hi, 16)],
                    local.at[kv],
                ).start()
        q_whole.append(pltpu.make_async_copy(q_hbm.at[:, cols], b["q"].at[kv], local.at[kv]))
    targets = [b["ck"], b["cv"], b["wall"].at[c, x], b["qk"], b["qv"], b["cq"]]
    sources = [inputs[1], inputs[2], inputs[6], inputs[4], inputs[5], inputs[3]]
    loads = [
        pltpu.make_async_copy(src, dst, local.at[i + 2])
        for i, (src, dst) in enumerate(zip(sources, targets))
    ]
    start(loads)
    anchor_ref, owner_ref, counts_ref = (b[n] for n in SCALARS)
    ints = [
        pltpu.make_async_copy(src, b[n], local.at[i + 8]) for i, (src, n) in enumerate(zip(scalars, SCALARS))
    ]
    start(ints)
    greet()
    for l in ints:
        l.wait()
    me = (x * NZ + z) * 2 + c
    own_count = counts_ref[me]
    is_owner = me == owner_ref[0]
    anchor_count = jnp.where(me == anchor_ref[0], 0, counts_ref[anchor_ref[0]])
    sems = Sems(b["send"], b["recv"])
    owner, anchor = coords(owner_ref[0]), coords(anchor_ref[0])
    qs = [
        Spread(sems, b["q"].at[i], b["qo"].at[i], *bufs[5 * i : 5 * i + 5], owner, XZ, True)
        for i in range(2)
    ]
    k = Spread(sems, b["ck"], b["ko"], *bufs[10:15], anchor, ZX, False)
    v = Spread(sems, b["cv"], b["vo"], *bufs[15:20], anchor, XZ, False)
    combs = [
        Combine(sems, *[b[n].at[i] for n in COMBINE_BUFFERS]) for i in range(2)
    ]
    shares = [Share(sems, b["attn"].at[i]) for i in range(2)]
    wall = b["wall"]
    w_copies = []

    def own(rb, first=0):
        @pl.loop(first, first + 1 if rb == 3 else LOCAL_KV)
        def _(kv):
            own_part(kv, rb, b["cq"], b["ka"], b["va"], b["o_own"], b["m_own"])

    def ask(kv):
        query_part(
            kv, b["qo"], b["ka"], b["va"], b["o_self"], b["m_self"], is_owner, b["part"], b["part32"]
        )
        combs[kv].step0()

    def slots(lo, hi):
        for i in range(lo, hi):
            anchor_part(
                i % 2, i // 2, b["cq"], b["kaa"], b["vaa"], b["o_own"], b["m_own"], out_vmem, own_count
            )

    def w_along_x():
        loads[2].wait()
        for d in range(1, NX):
            w_copies.append(sems.copy(wall.at[c, x], wall.at[c, x], {"blk_0": lax.rem(x + d, NX)}))
        start(w_copies)

    def w_to_core():
        arrived(w_copies)
        w_copies.append(sems.copy(wall.at[c], wall.at[c], {"blk_2": 1 - c}))
        w_copies[-1].start()

    for i in range(2):
        q_whole[i].wait()
        qs[i].step0()
    loads[0].wait()
    k.step0()
    loads[1].wait()
    v.step0()
    widen(b["ck"], b["cv"], b["ka"], b["va"], own_count)
    qs[0].step1()
    qs[1].step1()
    k.step1()
    v.step1()
    for l in loads[3:]:
        l.wait()
    widen(b["qk"], b["qv"], b["kqa"], b["vqa"], QT)
    own(0)

    @pl.loop(0, LOCAL_KV)
    def _(kv):
        self_part(kv, b["q"], b["kqa"], b["vqa"], b["o_self"], b["m_self"])

    qs[0].step2()
    qs[1].step2()
    own(1)
    own(2)
    qs[0].step3()
    qs[1].step3()
    own(3, 0)
    k.step2()
    v.step2()
    own(3, 1)
    qs[0].step4()
    qs[1].step4()
    k.step3()
    v.step3()
    qs[0].step5()
    qs[1].step5()
    k.step4()
    qs[0].step6()
    v.step4()
    ask(0)
    qs[1].step6()
    ask(1)
    combs[0].step1()
    combs[1].step1()
    v.step5()
    k.step5()
    v.step6()
    k.step6()
    widen(b["ko"], b["vo"], b["kaa"], b["vaa"], anchor_count)
    slots(0, 2)
    combs[0].step2()
    combs[1].step2()
    w_along_x()
    slots(2, 4)
    for cb, sh in zip(combs, shares):
        sh.out[sh.own()] = cb.step3()
        sh.share()
    w_to_core()
    slots(4, 6)
    shares[0].step6()
    shares[1].step6()
    arrived(w_copies[3:])
    project(b["attn"], wall, b["sb"])
    last = []
    for px, pc, py in plane_peers():
        to = {"blk_0": px, "blk_2": pc, "head": py}
        last.append(sems.copy(b["sb"].at[pc * NX + px], b["rf"].at[y, slot], to))
    start(last)
    b["rf"][y, slot] = b["sb"][slot]
    slots(6, 8)
    arrived(last)
    answer(b["rf"], ans)
    groups = [o.copies for o in (*qs, k, v, *combs, *shares)] + [w_copies, last]
    for group in groups:
        for cp in group:
            cp.wait_send()


COMBINE_BUFFERS = ("part", "part32", "r0", "p1", "p1f", "r1", "p2", "p2f", "s2", "r2o", "r2s")
VM = pl.BlockSpec(memory_space=pltpu.VMEM)
SM = pl.BlockSpec(memory_space=pltpu.SMEM)
HB = pl.BlockSpec(memory_space=pl.ANY)


def shape(*dims, dtype=BF16):
    return jax.ShapeDtypeStruct(dims, dtype)


def per_device(ctx_q, ctx_k, ctx_v, query_q, query_k, query_v, out_weight, anchor_index, owner_index, counts):
    spreads = (
        spread_scratch(QT, 512, XZ, True) * 2
        + spread_scratch(ROWS, 256, ZX, False)
        + spread_scratch(ROWS, 256, XZ, False)
    )
    ctx_out, ans = pl.pallas_call(
        layer_kernel,
        out_shape=(pltpu.VMEM((ROWS, 1024), BF16), pltpu.VMEM((64, QT), BF16)),
        in_specs=[HB] * 10,
        out_specs=(VM, VM),
        scratch_shapes=list(scratch_list().values()) + spreads,
        compiler_params=pltpu.CompilerParams(collective_id=0, has_side_effects=True, vmem_limit_bytes=VMEM_LIMIT),
        name="layer",
    )(
        anchor_index, owner_index, counts, query_q[0], ctx_k, ctx_v, ctx_q, query_k[0], query_v[0], out_weight.T
    )
    return ctx_out, ans.T


def solution(mesh):
    torus = Mesh(
        mesh.devices.reshape(NX, NZ, 2, mesh.shape["head"]), ("blk_0", "blk_1", "blk_2", "head")
    )
    placed = (
        P(BLK, "head"),
        P(BLK, "head"),
        P(BLK, "head"),
        P(BLK, None, "head"),
        P(BLK, None, "head"),
        P(BLK, None, "head"),
        P("head", BLK),
        P(),
        P(),
        P(),
    )
    return jax.shard_map(
        per_device,
        mesh=torus,
        in_specs=placed,
        out_specs=(P(BLK, "head"), P(None, BLK)),
        check_vma=False,
    )
```

time: 120 us -> 73.1 us (0.61)
  Pallas kernels: 115 us -> 69.2 us
    pallas_call x3 -> x1, Pallas kernels: 115 us -> 69.2 us  [per_device(): pl.pallas_call(layer_kernel, out_shape=(pltpu.VMEM((ROWS, 1024), BF16), p...]
where the time goes in v2:
time: 73.1 us; the launch traced here: 73 us
  Pallas kernels  69.2 us (95%)
  local copies, waits for them, and re-layouts  1.94 us (3%)
  between operations  1.93 us (3%)
    pallas_call x1, Pallas kernels, per_device(): pl.pallas_call(layer_kernel, out_shape=(pltpu.VMEM((ROWS, 1024), BF16), p...  69.2 us
    unnamed x2, local copies, waits for them, and re-layouts  1.94 us

profile of v2, /device:TPU:1, one launch (start us, length us, event | category | flops | bytes accessed | tf_op | source)
XLA Modules:
  0.0 73.0 jit_solution(7311837368635159630)
XLA Ops:
  1.9 69.2 %layer.1 = (bf16[1024,1024]{1,0:T(8,128)(2,1)S(1)}, bf16[64,256]{1,0:T(8,128)(2,1)S(1)}) custom-call(s32[1]{0:T(128)S(6)} %copy.16.refs_0_, s32[1]{0:T(128)S(6)} %copy.17.refs_1_, s32[64]{0:T(128)} %refs_2_.1, bf16[256,1024]{1,0:T(8,128)(2,1)} %bitcast.6, bf16[1024,256]{1,0:T(8,128)(2,1)} %refs_4_.1, bf16[1024,256]{1,0:T(8,128)(2,1)} %refs_5_.1, ...), custom_call_target="tpu_custom_call" | custom-call | tf_op jit(solution)/shard_map/layer/pallas_call | solution.py:670
  71.1 1.3 %copy.14 = bf16[1024,1024]{1,0:T(8,128)(2,1)} copy(bf16[1024,1024]{1,0:T(8,128)(2,1)S(1)} %get-tuple-element.6) | data formatting | bytes 4194304
  72.4 0.6 copy.15

commit v3 on v2

--- a/solution.py
+++ b/solution.py
@@ -56,29 +56,36 @@
 class Sems:
     def __init__(self, send, recv):
         self.send, self.recv, self.used = send, recv, 0
-
-    def copy(self, src, dst, target):
+        self.groups = []
+
+    def go(self, copies, region):
         i = self.used
         self.used += 1
-        return pltpu.make_async_remote_copy(
-            src_ref=src,
-            dst_ref=dst,
-            send_sem=self.send.at[i],
-            recv_sem=self.recv.at[i],
-            device_id=target,
-            device_id_type=MESH_ID,
-        )
+
+        def remote(src, dst, target):
+            return pltpu.make_async_remote_copy(
+                src_ref=src,
+                dst_ref=dst,
+                send_sem=self.send.at[i],
+                recv_sem=self.recv.at[i],
+                device_id=target,
+                device_id_type=MESH_ID,
+            )
+
+        for src, dst, target in copies:
+            remote(src, dst, target).start()
+        whole = remote(region, region, copies[0][2])
+        self.groups.append(whole)
+        return whole
+
+    def finish(self):
+        for whole in self.groups:
+            whole.wait_send()
 
 
 def start(copies):
     for c in copies:
         c.start()
-    return copies
-
-
-def arrived(copies):
-    for c in copies:
-        c.wait_recv()
 
 
 def zslice(z):
@@ -106,7 +113,6 @@
         self.me = {"blk_0": x, "blk_1": z}
         self.first, self.second = order
         self.part = half // SIZE[self.first]
-        self.copies = []
 
     def peers(self, axis):
         return [lax.rem(self.me[axis] + d, SIZE[axis]) for d in range(1, SIZE[axis])]
@@ -122,36 +128,38 @@
             return zslice(i)
         return rows_at(16 * i, 16), pl.ds(0, 256)
 
-    def go(self, copies):
-        self.copies += copies
-        self.now = start(copies)
+    def some(self, slots, axis):
+        return slots.at[0 : SIZE[axis] - 1]
 
     def step0(self):
         other = 1 - self.c
-        self.go([self.sems.copy(self.src.at[self.rows_half(other)], self.s0.at[self.c], {"blk_2": other})])
+        copy = (self.src.at[self.rows_half(other)], self.s0.at[self.c], {"blk_2": other})
+        self.now = self.sems.go([copy], self.s0.at[0])
         self.s0[self.c] = self.src[self.rows_half(self.c), :]
 
     def step1(self):
-        arrived(self.now)
+        self.now.wait_recv()
         self.c1[...] = self.s0[self.source["blk_2"]]
         i = self.me[self.first]
-        self.go(
+        self.now = self.sems.go(
             [
-                self.sems.copy(self.c1.at[self.rows_part(0, t)], self.sx.at[i], {self.first: t})
+                (self.c1.at[self.rows_part(0, t)], self.sx.at[i], {self.first: t})
                 for t in self.peers(self.first)
-            ]
+            ],
+            self.some(self.sx, self.first),
         )
         self.sx[i] = self.c1[self.rows_part(0, i), :]
 
     def step2(self):
-        arrived(self.now)
+        self.now.wait_recv()
         self.c2[...] = self.sx[self.source[self.first]]
         i = self.me[self.second]
-        self.go(
+        self.now = self.sems.go(
             [
-                self.sems.copy(self.c2.at[self.slice2(t)], self.sz.at[i], {self.second: t})
+                (self.c2.at[self.slice2(t)], self.sz.at[i], {self.second: t})
                 for t in self.peers(self.second)
-            ]
+            ],
+            self.some(self.sz, self.second),
         )
         self.sz[i] = self.c2[self.slice2(i)]
 
@@ -163,26 +171,32 @@
         return rows_at(base + 16 * i, 16), pl.ds(0, 256)
 
     def step3(self):
-        arrived(self.now)
+        self.now.wait_recv()
         self.out[self.own()] = self.sz[self.source[self.second]]
         self.share()
 
+    sz = sx = None
+
     def share(self):
         piece = self.out.at[self.own()]
-        self.go([self.sems.copy(piece, piece, {self.second: t}) for t in self.peers(self.second)])
+        self.now = self.sems.go(
+            [(piece, piece, {self.second: t}) for t in self.peers(self.second)], self.some(self.sz, self.second)
+        )
 
     def step4(self):
-        arrived(self.now)
+        self.now.wait_recv()
         piece = self.out.at[self.rows_part(self.c, self.me[self.first])]
-        self.go([self.sems.copy(piece, piece, {self.first: t}) for t in self.peers(self.first)])
+        self.now = self.sems.go(
+            [(piece, piece, {self.first: t}) for t in self.peers(self.first)], self.some(self.sx, self.first)
+        )
 
     def step5(self):
-        arrived(self.now)
+        self.now.wait_recv()
         piece = self.out.at[self.rows_half(self.c)]
-        self.go([self.sems.copy(piece, piece, {"blk_2": 1 - self.c})])
+        self.now = self.sems.go([(piece, piece, {"blk_2": 1 - self.c})], self.s0.at[0])
 
     def step6(self):
-        arrived(self.now)
+        self.now.wait_recv()
 
 
 def coords(i):
@@ -350,18 +364,14 @@
         self.r0, self.p1, self.p1f, self.r1 = r0, p1, p1f, r1
         self.p2, self.p2f, self.s2, self.r2o, self.r2s = p2, p2f, s2, r2o, r2s
         self.x, self.z, self.c, self.y = where_am_i()
-        self.copies = []
-
-    def go(self, copies):
-        self.copies += copies
-        self.now = start(copies)
 
     def step0(self):
         other = 1 - self.c
-        self.go([self.sems.copy(self.part.at[rows_at(128 * other, 128)], self.r0, {"blk_2": other})])
+        copy = (self.part.at[rows_at(128 * other, 128)], self.r0, {"blk_2": other})
+        self.now = self.sems.go([copy], self.r0)
 
     def step1(self):
-        arrived(self.now)
+        self.now.wait_recv()
 
         @pl.loop(0, 4)
         def _(i):
@@ -380,11 +390,11 @@
         out = []
         for d in range(1, NX):
             t = lax.rem(self.x + d, NX)
-            out.append(self.sems.copy(self.p1.at[rows_at(32 * t, 32)], self.r1.at[d - 1], {"blk_0": t}))
-        self.go(out)
+            out.append((self.p1.at[rows_at(32 * t, 32)], self.r1.at[d - 1], {"blk_0": t}))
+        self.now = self.sems.go(out, self.r1)
 
     def step2(self):
-        arrived(self.now)
+        self.now.wait_recv()
         mine = rows_at(32 * self.x, 32)
         outs, lse = merge(
             [heads_of(self.p1f, mine)] + [heads_of(self.r1.at[i], slice(0, 32)) for i in range(NX - 1)],
@@ -396,16 +406,18 @@
             self.p2f[:, h * 128 : h * 128 + 128] = o
         for g in range(4):
             self.s2[g] = pack_stat(pltpu.roll(lse, 128 - g, 1) if g else lse)
-        out = []
+        stats, out = [], []
         for d in range(1, NZ):
             t = lax.rem(self.z + d, NZ)
             rows, cols = zslice(t)
-            out.append(self.sems.copy(self.p2.at[rows, cols], self.r2o.at[d - 1], {"blk_1": t}))
-            out.append(self.sems.copy(self.s2.at[lax.rem(t, 4), rows], self.r2s.at[d - 1], {"blk_1": t}))
-        self.go(out)
+            stats.append((self.s2.at[lax.rem(t, 4), rows], self.r2s.at[d - 1], {"blk_1": t}))
+            out.append((self.p2.at[rows, cols], self.r2o.at[d - 1], {"blk_1": t}))
+        self.now_stats = self.sems.go(stats, self.r2s)
+        self.now = self.sems.go(out, self.r2o)
 
     def step3(self):
-        arrived(self.now)
+        self.now_stats.wait_recv()
+        self.now.wait_recv()
         rows, cols = zslice(self.z)
         own = self.p2f[rows, cols]
         outs, _ = merge(
@@ -418,12 +430,15 @@
 
 
 class Share(Spread):
-    def __init__(self, sems, out):
-        self.sems, self.out = sems, out
+    def __init__(self, sems, out, slots):
+        self.sems, self.out, self.slots = sems, out, slots
         self.setup(("blk_0", "blk_1"), True, 128)
 
     def own(self):
         return zslice(self.me["blk_1"])
+
+    def some(self, slots, axis):
+        return self.slots
 
 
 def project(attn, wall, sb):
@@ -435,7 +450,7 @@
 
 
 def answer(rf, ans):
-    total = (((rf[0] + rf[1]) + rf[2]) + rf[3]).reshape(128, 128).T
+    total = (((rf[0:8] + rf[8:16]) + rf[16:24]) + rf[24:32]).reshape(128, 128).T
     ans[:, 0:128] = total[0:64].astype(BF16)
     ans[:, 128:256] = total[64:128].astype(BF16)
 
@@ -444,7 +459,7 @@
 ZX = ("blk_1", "blk_0")
 N_LOCAL = 11
 SCALARS = ("anchor", "owner", "counts")
-N_REMOTE = 4 * 22 + 2 * (1 + 3 + 14 + 7) + 4 + 31
+N_REMOTE = 4 * 6 + 2 * (4 + 1) + 3
 
 
 def scratch_list():
@@ -479,7 +494,7 @@
         r2s=pltpu.VMEM((2, NZ - 1, 16, 128), BF16),
         attn=pltpu.VMEM((2, 32, 512), BF16),
         sb=pltpu.VMEM((8, 16, 128), F32),
-        rf=pltpu.VMEM((NY, 8, 16, 128), F32),
+        rf=pltpu.VMEM((NY * 8, 16, 128), F32),
         anchor=pltpu.SMEM((1,), jnp.int32),
         owner=pltpu.SMEM((1,), jnp.int32),
         counts=pltpu.SMEM((64,), jnp.int32),
@@ -540,7 +555,7 @@
     combs = [
         Combine(sems, *[b[n].at[i] for n in COMBINE_BUFFERS]) for i in range(2)
     ]
-    shares = [Share(sems, b["attn"].at[i]) for i in range(2)]
+    shares = [Share(sems, b["attn"].at[i], b["r2o"].at[i]) for i in range(2)]
     wall = b["wall"]
     w_copies = []
 
@@ -563,14 +578,13 @@
 
     def w_along_x():
         loads[2].wait()
-        for d in range(1, NX):
-            w_copies.append(sems.copy(wall.at[c, x], wall.at[c, x], {"blk_0": lax.rem(x + d, NX)}))
-        start(w_copies)
+        mine = wall.at[c, x]
+        to = [(mine, mine, {"blk_0": lax.rem(x + d, NX)}) for d in range(1, NX)]
+        w_copies.append(sems.go(to, wall.at[0, 0:3]))
 
     def w_to_core():
-        arrived(w_copies)
-        w_copies.append(sems.copy(wall.at[c], wall.at[c], {"blk_2": 1 - c}))
-        w_copies[-1].start()
+        w_copies[0].wait_recv()
+        w_copies.append(sems.go([(wall.at[c], wall.at[c], {"blk_2": 1 - c})], wall.at[0]))
 
     for i in range(2):
         q_whole[i].wait()
@@ -634,21 +648,18 @@
     slots(4, 6)
     shares[0].step6()
     shares[1].step6()
-    arrived(w_copies[3:])
+    w_copies[1].wait_recv()
     project(b["attn"], wall, b["sb"])
     last = []
     for px, pc, py in plane_peers():
         to = {"blk_0": px, "blk_2": pc, "head": py}
-        last.append(sems.copy(b["sb"].at[pc * NX + px], b["rf"].at[y, slot], to))
-    start(last)
-    b["rf"][y, slot] = b["sb"][slot]
+        last.append((b["sb"].at[pc * NX + px], b["rf"].at[y * 8 + slot], to))
+    final = sems.go(last, b["rf"].at[0:31])
+    b["rf"][y * 8 + slot] = b["sb"][slot]
     slots(6, 8)
-    arrived(last)
+    final.wait_recv()
     answer(b["rf"], ans)
-    groups = [o.copies for o in (*qs, k, v, *combs, *shares)] + [w_copies, last]
-    for group in groups:
-        for cp in group:
-            cp.wait_send()
+    sems.finish()
 
 
 COMBINE_BUFFERS = ("part", "part32", "r0", "p1", "p1f", "r1", "p2", "p2f", "s2", "r2o", "r2s")

time: 73.1 us -> 70.4 us (0.963)
  Pallas kernels: 69.2 us -> 66.5 us
    pallas_call x1, Pallas kernels: 69.2 us -> 66.5 us  [per_device(): pl.pallas_call(layer_kernel, out_shape=(pltpu.VMEM((ROWS, 1024), BF16), p...]
where the time goes in v3:
time: 70.4 us; the launch traced here: 70.3 us
  Pallas kernels  66.5 us (94%)
  local copies, waits for them, and re-layouts  1.94 us (3%)
  between operations  1.93 us (3%)
    pallas_call x1, Pallas kernels, per_device(): pl.pallas_call(layer_kernel, out_shape=(pltpu.VMEM((ROWS, 1024), BF16), p...  66.5 us
    unnamed x2, local copies, waits for them, and re-layouts  1.94 us

profile of v3, /device:TPU:1, one launch (start us, length us, event | category | flops | bytes accessed | tf_op | source)
XLA Modules:
  0.0 70.3 jit_solution(2416049957274579833)
XLA Ops:
  1.9 66.5 %layer.1 = (bf16[1024,1024]{1,0:T(8,128)(2,1)S(1)}, bf16[64,256]{1,0:T(8,128)(2,1)S(1)}) custom-call(s32[1]{0:T(128)S(6)} %copy.16.refs_0_, s32[1]{0:T(128)S(6)} %copy.17.refs_1_, s32[64]{0:T(128)} %refs_2_.1, bf16[256,1024]{1,0:T(8,128)(2,1)} %bitcast.6, bf16[1024,256]{1,0:T(8,128)(2,1)} %refs_4_.1, bf16[1024,256]{1,0:T(8,128)(2,1)} %refs_5_.1, ...), custom_call_target="tpu_custom_call" | custom-call | tf_op jit(solution)/shard_map/layer/pallas_call | solution.py:681
  68.4 1.3 %copy.14 = bf16[1024,1024]{1,0:T(8,128)(2,1)} copy(bf16[1024,1024]{1,0:T(8,128)(2,1)S(1)} %get-tuple-element.6) | data formatting | bytes 4194304
  69.7 0.6 copy.15

commit v4 on v3

--- a/solution.py
+++ b/solution.py
@@ -446,11 +446,12 @@
     p = nt(rows, wall[...].reshape(512, 1024))
     for i in range(8):
         cols = slice(i * 64, i * 64 + 64)
-        sb[i] = jnp.concatenate([p[0:16, cols], p[16:32, cols]], axis=1)
+        sb[i] = jnp.concatenate([p[0:16, cols], p[16:32, cols]], axis=1).astype(BF16)
 
 
 def answer(rf, ans):
-    total = (((rf[0:8] + rf[8:16]) + rf[16:24]) + rf[24:32]).reshape(128, 128).T
+    parts = [rf[8 * i : 8 * i + 8].astype(F32) for i in range(NY)]
+    total = (((parts[0] + parts[1]) + parts[2]) + parts[3]).reshape(128, 128).T
     ans[:, 0:128] = total[0:64].astype(BF16)
     ans[:, 128:256] = total[64:128].astype(BF16)
 
@@ -493,8 +494,8 @@
         r2o=pltpu.VMEM((2, NZ - 1, 16, 128), BF16),
         r2s=pltpu.VMEM((2, NZ - 1, 16, 128), BF16),
         attn=pltpu.VMEM((2, 32, 512), BF16),
-        sb=pltpu.VMEM((8, 16, 128), F32),
-        rf=pltpu.VMEM((NY * 8, 16, 128), F32),
+        sb=pltpu.VMEM((8, 16, 128), BF16),
+        rf=pltpu.VMEM((NY * 8, 16, 128), BF16),
         anchor=pltpu.SMEM((1,), jnp.int32),
         owner=pltpu.SMEM((1,), jnp.int32),
         counts=pltpu.SMEM((64,), jnp.int32),
@@ -597,7 +598,6 @@
     qs[0].step1()
     qs[1].step1()
     k.step1()
-    v.step1()
     for l in loads[3:]:
         l.wait()
     widen(b["qk"], b["qv"], b["kqa"], b["vqa"], QT)
@@ -609,6 +609,7 @@
 
     qs[0].step2()
     qs[1].step2()
+    v.step1()
     own(1)
     own(2)
     qs[0].step3()

time: 70.4 us -> 69.9 us (level)
  no operation moved by 1% of the time
where the time goes in v4:
time: 69.9 us; the launch traced here: 69.8 us
  Pallas kernels  65.9 us (94%)
  local copies, waits for them, and re-layouts  1.94 us (3%)
  between operations  1.93 us (3%)
    pallas_call x1, Pallas kernels, per_device(): pl.pallas_call(layer_kernel, out_shape=(pltpu.VMEM((ROWS, 1024), BF16), p...  65.9 us
    unnamed x2, local copies, waits for them, and re-layouts  1.94 us

profile of v4, /device:TPU:1, one launch (start us, length us, event | category | flops | bytes accessed | tf_op | source)
XLA Modules:
  0.0 69.8 jit_solution(15390488843216661681)
XLA Ops:
  1.9 65.9 %layer.1 = (bf16[1024,1024]{1,0:T(8,128)(2,1)S(1)}, bf16[64,256]{1,0:T(8,128)(2,1)S(1)}) custom-call(s32[1]{0:T(128)S(6)} %copy.16.refs_0_, s32[1]{0:T(128)S(6)} %copy.17.refs_1_, s32[64]{0:T(128)} %refs_2_.1, bf16[256,1024]{1,0:T(8,128)(2,1)} %bitcast.6, bf16[1024,256]{1,0:T(8,128)(2,1)} %refs_4_.1, bf16[1024,256]{1,0:T(8,128)(2,1)} %refs_5_.1, ...), custom_call_target="tpu_custom_call" | custom-call | tf_op jit(solution)/shard_map/layer/pallas_call | solution.py:682
  67.9 1.3 %copy.14 = bf16[1024,1024]{1,0:T(8,128)(2,1)} copy(bf16[1024,1024]{1,0:T(8,128)(2,1)S(1)} %get-tuple-element.6) | data formatting | bytes 4194304
  69.2 0.6 copy.15
